TPU v7x, 32 devices: a whole 2x2x4 slice. The times are simulated.
32 devices in a mesh: ctx: 16 (over z, y, x), tp: 2 (over core).
Axes of the slice: x: 2, y: 2, z: 4, core: 2. Of those that a mesh axis runs over, the one named last changes fastest.
Arguments:
- rotated_asking_vectors: bfloat16 [2, 512, 64, 128], P(None, ('ctx', 'tp')), may hold values from -6 to 6
- rotated_match_vectors: bfloat16 [2, 512, 8, 128], P(None, ('ctx', 'tp')), may hold values from -6 to 6
- content_vectors: bfloat16 [2, 512, 8, 128], P(None, ('ctx', 'tp')), may hold values from -6 to 6
- result_cotangent: bfloat16 [2, 512, 64, 128], P(None, ('ctx', 'tp')), may hold values from -6 to 6
Outputs:
- attended: bfloat16 [2, 512, 64, 128], P(None, ('ctx', 'tp'))
- grad_query: bfloat16 [2, 512, 64, 128], P(None, ('ctx', 'tp'))
- grad_key: bfloat16 [2, 512, 8, 128], P(None, ('ctx', 'tp'))
- grad_value: bfloat16 [2, 512, 8, 128], P(None, ('ctx', 'tp'))
All inputs are finite; a program needn't handle non-finite values.
Results may differ from a plain program's by a relative error of at most 0.002.
Values may be sent and summed in bfloat16 or wider, within the bound.
A program may use at most 64 MiB of HBM per device.

v0:
```python
from functools import partial

import jax
import jax.numpy as jnp
from jax import lax
from jax.sharding import PartitionSpec as P

masked_score = -1e30


def folded(value, axis, dim, absorb, carry):
    whole = jax.tree.map(lambda part: lax.all_gather(part, axis, axis=dim, tiled=True), value)
    return absorb(carry, whole, jnp.int32(0))


def as_sent(value):
    return jax.tree.map(lambda a: a.astype(jnp.bfloat16) if a.dtype == jnp.float32 else a, value)


def add_rows(totals, piece, first_row):
    current = lax.dynamic_slice_in_dim(totals, first_row, piece.shape[0], 0)
    return lax.dynamic_update_slice_in_dim(totals, current + piece, first_row, 0)


def causal_scores(work_query, key_piece, first_row, positions, softmax_scale):
    piece_len = key_piece.shape[0]
    scores = (
        jnp.einsum("tkgd,nkd->tkgn", work_query, key_piece, preferred_element_type=jnp.float32)
        * softmax_scale
    )
    key_position = first_row + jnp.arange(piece_len, dtype=jnp.int32)
    allowed = (key_position[None, :] <= positions[:, None])[:, None, None, :]
    return (jnp.where(allowed, scores, masked_score), allowed)


def forward_step(state_now, pieces, first_row, work_query, positions, softmax_scale):
    key_piece, value_piece = pieces

    def update(state_in):
        weighted, run_max, run_sum = state_in
        scores, allowed = causal_scores(work_query, key_piece, first_row, positions, softmax_scale)
        new_max = jnp.maximum(run_max, jnp.max(scores, axis=-1))
        weights = jnp.where(allowed, jnp.exp(scores - new_max[..., None]), 0.0)
        factor = jnp.exp(run_max - new_max)
        weighted = weighted * factor[..., None] + jnp.einsum(
            "tkgn,nkd->tkgd",
            weights,
            value_piece.astype(jnp.float32),
            precision=lax.Precision.HIGHEST,
        )
        run_sum = run_sum * factor + jnp.sum(weights, axis=-1)
        return (weighted, new_max, run_sum)

    return lax.cond(first_row <= jnp.max(positions), update, lambda state_in: state_in, state_now)


def backward_step(
    state_now,
    pieces,
    first_row,
    work_query,
    expanded_asking_vectors,
    work_grad,
    expanded_cotangent,
    log_norm,
    row_delta,
    positions,
    softmax_scale,
):
    key_piece, value_piece = pieces

    def update(state_in):
        query_total, key_total, value_total = state_in
        scores, allowed = causal_scores(work_query, key_piece, first_row, positions, softmax_scale)
        probabilities = jnp.where(allowed, jnp.exp(scores - log_norm[..., None]), 0.0)
        prob_grad = jnp.einsum(
            "tkgd,nkd->tkgn", work_grad, value_piece, preferred_element_type=jnp.float32
        )
        dscore = probabilities * (prob_grad - row_delta[..., None])
        query_total = query_total + softmax_scale * jnp.einsum(
            "tkgn,nkd->tkgd", dscore, key_piece.astype(jnp.float32), precision=lax.Precision.HIGHEST
        )
        key_term = softmax_scale * jnp.einsum(
            "tkgn,tkgd->nkd", dscore, expanded_asking_vectors, precision=lax.Precision.HIGHEST
        )
        value_term = jnp.einsum(
            "tkgn,tkgd->nkd", probabilities, expanded_cotangent, precision=lax.Precision.HIGHEST
        )
        return (
            query_total,
            add_rows(key_total, key_term, first_row),
            add_rows(value_total, value_term, first_row),
        )

    return lax.cond(first_row <= jnp.max(positions), update, lambda state_in: state_in, state_now)


def on_device(rotated_asking_vectors, rotated_match_vectors, content_vectors, result_cotangent):
    query_heads, key_heads, value_heads, grad_heads = (
        lax.all_to_all(rotated_asking_vectors, "tp", split_axis=2, concat_axis=1, tiled=True),
        lax.all_to_all(rotated_match_vectors, "tp", split_axis=2, concat_axis=1, tiled=True),
        lax.all_to_all(content_vectors, "tp", split_axis=2, concat_axis=1, tiled=True),
        lax.all_to_all(result_cotangent, "tp", split_axis=2, concat_axis=1, tiled=True),
    )
    layer_count, tok_rows, head_count, head_depth = query_heads.shape
    kv_heads = key_heads.shape[2]
    group_size = head_count // kv_heads
    ctx_count = lax.axis_size("ctx")
    ctx_rank = lax.axis_index("ctx")
    softmax_scale = head_depth ** (-0.5)
    total_rows = ctx_count * tok_rows
    own_rows = ctx_rank * tok_rows + jnp.arange(tok_rows, dtype=jnp.int32)
    work_queries, work_grads, positions = (query_heads, grad_heads, own_rows)
    attended_list, query_grads, key_parts, value_parts = ([], [], [], [])
    lead_shape = (tok_rows, kv_heads, group_size)
    for depth_position in range(layer_count):
        work_query = work_queries[depth_position].reshape(lead_shape + (head_depth,))
        work_grad = work_grads[depth_position].reshape(lead_shape + (head_depth,))
        forward_init = (
            jnp.zeros(lead_shape + (head_depth,), jnp.float32),
            jnp.full(lead_shape, masked_score, jnp.float32),
            jnp.zeros(lead_shape, jnp.float32),
        )
        forward_fn = partial(
            forward_step, work_query=work_query, positions=positions, softmax_scale=softmax_scale
        )
        weighted, run_max, run_sum = folded(
            (key_heads[depth_position], value_heads[depth_position]),
            "ctx",
            0,
            forward_fn,
            forward_init,
        )
        attended_now = (weighted / run_sum[..., None]).astype(jnp.bfloat16)
        log_norm = run_max + jnp.log(run_sum)
        saved_out = lax.optimization_barrier(attended_now).astype(jnp.float32)
        expanded_cotangent = work_grad.astype(jnp.float32)
        row_delta = jnp.sum(expanded_cotangent * saved_out, axis=-1)
        expanded_asking_vectors = work_query.astype(jnp.float32)
        backward_init = (
            jnp.zeros(lead_shape + (head_depth,), jnp.float32),
            jnp.zeros((total_rows, kv_heads, head_depth), jnp.float32),
            jnp.zeros((total_rows, kv_heads, head_depth), jnp.float32),
        )
        backward_fn = partial(
            backward_step,
            work_query=work_query,
            expanded_asking_vectors=expanded_asking_vectors,
            work_grad=work_grad,
            expanded_cotangent=expanded_cotangent,
            log_norm=log_norm,
            row_delta=row_delta,
            positions=positions,
            softmax_scale=softmax_scale,
        )
        query_total, key_total, value_total = folded(
            (key_heads[depth_position], value_heads[depth_position]),
            "ctx",
            0,
            backward_fn,
            backward_init,
        )
        attended_list.append(attended_now.reshape(tok_rows, head_count, head_depth))
        query_grads.append(
            query_total.astype(jnp.bfloat16).reshape(tok_rows, head_count, head_depth)
        )
        key_parts.append(key_total)
        value_parts.append(value_total)
    key_sum, value_sum = (
        lax.psum_scatter(jnp.stack(key_parts), "ctx", scatter_dimension=1, tiled=True),
        lax.psum_scatter(jnp.stack(value_parts), "ctx", scatter_dimension=1, tiled=True),
    )
    attended = jnp.stack(attended_list)
    grad_query = jnp.stack(query_grads)
    return (
        lax.all_to_all(as_sent(attended), "tp", split_axis=1, concat_axis=2, tiled=True).astype(
            attended.dtype
        ),
        lax.all_to_all(as_sent(grad_query), "tp", split_axis=1, concat_axis=2, tiled=True).astype(
            grad_query.dtype
        ),
        lax.all_to_all(key_sum.astype(jnp.bfloat16), "tp", split_axis=1, concat_axis=2, tiled=True),
        lax.all_to_all(
            value_sum.astype(jnp.bfloat16), "tp", split_axis=1, concat_axis=2, tiled=True
        ),
    )


def solution(mesh):
    return jax.shard_map(
        on_device,
        mesh=mesh,
        in_specs=(
            P(None, ("ctx", "tp"), None, None),
            P(None, ("ctx", "tp"), None, None),
            P(None, ("ctx", "tp"), None, None),
            P(None, ("ctx", "tp"), None, None),
        ),
        out_specs=(
            P(None, ("ctx", "tp"), None, None),
            P(None, ("ctx", "tp"), None, None),
            P(None, ("ctx", "tp"), None, None),
            P(None, ("ctx", "tp"), None, None),
        ),
        check_vma=False,
    )
```

profile of v0, /device:TPU:0, one launch (start us, length us, event | category | flops | bytes accessed | tf_op | source)
XLA Modules:
  0.0 441.4 jit_solution(6880946176727187239)
XLA Ops:
  0.6 1.5 copy.85
  2.1 3.3 all-to-all-start
  6.7 1.5 copy.89
  8.2 3.3 all-to-all-start.2
  11.6 2.2 copy.87
  13.8 3.5 all-to-all-start.1
  17.3 47.6 %all_gather.19 = bf16[512,4,128]{2,0,1:T(8,128)(2,1)} all-gather(bf16[32,4,128]{2,0,1:T(8,128)(2,1)S(1)} %bitcast.235), channel_id=1, replica_groups=mesh['ctx'=16,'tp'=2] {'ctx'}, dimensions={0}, use_global_device_ids=true | all-gather | bytes 557056 | tf_op jit(solution)/shard_map/all_gather | solution.py:12
  64.9 38.4 %all_gather.17 = bf16[512,4,128]{2,0,1:T(8,128)(2,1)S(1)} all-gather(bf16[32,4,128]{2,0,1:T(8,128)(2,1)S(1)} %bitcast.234), channel_id=1, replica_groups=mesh['ctx'=16,'tp'=2] {'ctx'}, dimensions={0}, use_global_device_ids=true | all-gather | bytes 557056 | tf_op jit(solution)/shard_map/all_gather | solution.py:12
  103.3 40.9 %all_gather.18 = bf16[512,4,128]{2,0,1:T(8,128)(2,1)S(1)} all-gather(bf16[32,4,128]{2,0,1:T(8,128)(2,1)S(1)} %bitcast.233), channel_id=1, replica_groups=mesh['ctx'=16,'tp'=2] {'ctx'}, dimensions={0}, use_global_device_ids=true | all-gather | bytes 557056 | tf_op jit(solution)/shard_map/all_gather | solution.py:12
  144.2 38.7 %all_gather.16 = bf16[512,4,128]{2,0,1:T(8,128)(2,1)S(1)} all-gather(bf16[32,4,128]{2,0,1:T(8,128)(2,1)S(1)} %bitcast.232), channel_id=1, replica_groups=mesh['ctx'=16,'tp'=2] {'ctx'}, dimensions={0}, use_global_device_ids=true | all-gather | bytes 557056 | tf_op jit(solution)/shard_map/all_gather | solution.py:12
  182.9 1.1 copy.98
  184.1 3.5 all-to-all-start.4
  188.4 6.8 %conditional.5 = (f32[32,4,8,128]{3,0,2,1:T(8,128)S(1)}, f32[32,4,8]{0,2,1:T(8,128)}, f32[32,4,8]{0,2,1:T(8,128)S(1)}, f32[32,4,8]{0,2,1:T(8,128)S(1)}) conditional(s32[]{:T(128)} %convert_element_type.74, () %tuple.70, (s32[32]{0:T(128)S(1)}, bf16[512,4,128]{2,0,1:T(8,128)(2,1)S(1)}, bf16[32,4,8,128]{3,0,2,1:T(8,128)(2,1)}, ...), branch_computations={%region_5.6_spmd, %region_6.9_spmd} | conditional | flops 945967104 | bytes 8241312 | solution.py:54
  188.4 1.5 fusion.17
  190.5 2.6 fusion.21
  193.1 1.4 fusion.18
  194.4 0.7 fusion.59
  195.4 5.5 %conditional.4 = (f32[32,4,8,128]{3,0,2,1:T(8,128)S(1)}, f32[32,4,8]{0,2,1:T(8,128)}, f32[32,4,8]{0,2,1:T(8,128)S(1)}, f32[32,4,8]{0,2,1:T(8,128)S(1)}) conditional(s32[]{:T(128)} %convert_element_type.74, () %tuple.68, (s32[32]{0:T(128)S(1)}, bf16[512,4,128]{2,0,1:T(8,128)(2,1)S(1)}, bf16[32,4,8,128]{3,0,2,1:T(8,128)(2,1)S(1)}, ...), branch_computations={%region_1.0_spmd, %region_2.5_spmd} | conditional | flops 945967104 | bytes 8241312 | solution.py:54
  196.6 2.2 fusion.4
  198.9 1.4 fusion.1
  200.2 0.7 fusion.57
  202.6 0.9 convert_element_type.78
  203.5 0.9 convert_element_type.77
  204.4 0.8 pad_maximum_fusion.2
  205.2 4.2 all-to-all-start.3
  209.6 13.0 %conditional.7 = (bf16[1,32,32,128]{3,2,1,0:T(8,128)(2,1)S(1)}, f32[1,512,4,128]{3,2,0,1:T(4,128)S(1)}, f32[1,512,4,128]{3,2,0,1:T(4,128)S(1)}) conditional(s32[]{:T(128)} %convert_element_type.74, () %tuple.74, (s32[32]{0:T(128)S(1)}, bf16[512,4,128]{2,0,1:T(8,128)(2,1)S(1)}, bf16[32,4,8,128]{3,0,2,1:T(8,128)(2,1)}, f32[32,4,8]{0,2,1:T(8,128)}, ...), branch_computations={%region_12.0_spmd, %region_13.15_spmd} | conditional | flops 2688434176 | bytes 24699032 | solution.py:95
  211.0 1.3 multiply_reduce_fusion.1
  212.3 1.6 fusion.48
  213.9 1.9 convolution_bitcast_fusion.2
  215.8 1.5 fusion.45
  217.2 1.1 fusion.52
  218.4 2.8 fusion.50
  223.7 10.8 %conditional.6 = (bf16[1,32,32,128]{3,2,1,0:T(8,128)(2,1)S(1)}, f32[1,512,4,128]{3,2,0,1:T(4,128)}, f32[1,512,4,128]{3,2,0,1:T(4,128)S(1)}) conditional(s32[]{:T(128)} %convert_element_type.74, () %tuple.72, (s32[32]{0:T(128)S(1)}, bf16[512,4,128]{2,0,1:T(8,128)(2,1)S(1)}, bf16[32,4,8,128]{3,0,2,1:T(8,128)(2,1)S(1)}, f32[32,4,8]{0,2,1:T(8,128)}, ...), branch_computations={%region_9.10_spmd, %region_10.0_spmd} | conditional | flops 2688434176 | bytes 24699032 | solution.py:95
  224.9 1.3 multiply_reduce_fusion
  226.8 1.9 convolution_bitcast_fusion
  229.1 1.1 fusion.41
  230.2 1.9 fusion.39
  232.1 1.7 copy.125
  234.6 2.0 pad_maximum_fusion.3
  236.6 4.2 all-to-all-start.5
  240.8 1.9 copy.97
  242.8 4.1 pad_maximum_fusion
  246.9 181.7 %all-reduce.4 = (bf16[2,512,4,128]{3,2,0,1:T(4,128)(2,1)S(1)}, bf16[2,512,4,128]{3,2,0,1:T(4,128)(2,1)}) all-reduce(f32[2,512,4,128]{3,2,0,1:T(4,128)S(1)} %get-tuple-element.308, f32[2,512,4,128]{3,2,0,1:T(4,128)} %get-tuple-element.309), channel_id=2, replica_groups=mesh['ctx'=16,'tp'=2] {'ctx'}, use_global_device_ids=true, to_apply=%region_15.16.clone | all-reduce | flops 1048576 | bytes 6291456
  428.6 1.5 dynamic-slice_convert_fusion
  430.1 3.3 all-to-all-start.7
  433.4 1.9 copy.104
  436.0 3.3 all-to-all-start.6
  440.0 0.7 all-to-all-done.6
  (56 shorter events, 13.4 us)
Async XLA Ops:
  2.1 6.1 %all-to-all-start = ((bf16[2,16,8,128]{3,1,0,2:T(8,128)(2,1)}), bf16[2,16,8,128]{3,1,0,2:T(8,128)(2,1)S(1)}, u32[]{:S(2)}, u32[]{:S(2)}) async-start(bf16[2,16,8,128]{3,1,0,2:T(8,128)(2,1)} %copy.85), calls=%async_computation | async-start | bytes 131072 | tf_op jit(solution)/shard_map/all_to_all | solution.py:101
  8.2 5.6 %all-to-all-start.2 = ((bf16[2,16,8,128]{3,1,0,2:T(8,128)(2,1)}), bf16[2,16,8,128]{3,1,0,2:T(8,128)(2,1)S(1)}, u32[]{:S(2)}, u32[]{:S(2)}) async-start(bf16[2,16,8,128]{3,1,0,2:T(8,128)(2,1)} %copy.89), calls=%async_computation.2 | async-start | bytes 131072 | tf_op jit(solution)/shard_map/all_to_all | solution.py:102
  11.5 171.4 %copy-start.3 = (bf16[2,16,64,128]{3,2,1,0:T(8,128)(2,1)S(1)}, bf16[2,16,64,128]{3,2,1,0:T(8,128)(2,1)}, u32[]{:S(2)}) copy-start(bf16[2,16,64,128]{3,2,1,0:T(8,128)(2,1)} %param.15) | copy-start | bytes 1572868
  13.8 170.3 %all-to-all-start.1 = ((bf16[2,16,64,128]{3,1,0,2:T(8,128)(2,1)}), bf16[2,16,64,128]{3,1,0,2:T(8,128)(2,1)S(1)}, u32[]{:S(2)}, u32[]{:S(2)}) async-start(bf16[2,16,64,128]{3,1,0,2:T(8,128)(2,1)} %copy.87), calls=%async_computation.1 | async-start | bytes 1048576 | tf_op jit(solution)/shard_map/all_to_all | solution.py:100
  184.1 21.1 %all-to-all-start.4 = ((bf16[2,16,64,128]{3,1,0,2:T(8,128)(2,1)}), bf16[2,16,64,128]{3,1,0,2:T(8,128)(2,1)S(1)}, u32[]{:S(2)}, u32[]{:S(2)}) async-start(bf16[2,16,64,128]{3,1,0,2:T(8,128)(2,1)} %copy.98), calls=%async_computation.4 | async-start | bytes 1048576 | tf_op jit(solution)/shard_map/all_to_all | solution.py:103
  195.4 6.0 %copy-start.4 = (u32[32]{0:T(128)S(1)}, u32[32]{0:T(128)}, u32[]{:S(2)}) copy-start(u32[32]{0:T(128)} %constant.95) | copy-start | bytes 388
  205.2 31.4 %all-to-all-start.3 = ((bf16[2,32,32,128]{3,2,0,1:T(8,128)(2,1)}), bf16[2,32,32,128]{3,2,0,1:T(8,128)(2,1)}, u32[]{:S(2)}, u32[]{:S(2)}) async-start(bf16[2,32,32,128]{3,2,0,1:T(8,128)(2,1)} %pad_maximum_fusion.2), calls=%async_computation.3 | async-start | bytes 1048576 | tf_op jit(solution)/shard_map/all_to_all | solution.py:176
  222.7 0.7 copy-start.2
  222.7 1.0 copy-start
  234.6 8.2 %copy-start.1 = (f32[1,512,4,128]{3,2,0,1:T(4,128)}, f32[1,512,4,128]{3,2,0,1:T(4,128)S(1)}, u32[]{:S(2)}) copy-start(f32[1,512,4,128]{3,2,0,1:T(4,128)S(1)} %get-tuple-element.283) | copy-start | bytes 3145732
  236.6 193.5 %all-to-all-start.5 = ((bf16[2,32,32,128]{3,2,0,1:T(8,128)(2,1)}), bf16[2,32,32,128]{3,2,0,1:T(8,128)(2,1)}, u32[]{:S(2)}, u32[]{:S(2)}) async-start(bf16[2,32,32,128]{3,2,0,1:T(8,128)(2,1)} %pad_maximum_fusion.3), calls=%async_computation.5 | async-start | bytes 1048576 | tf_op jit(solution)/shard_map/all_to_all | solution.py:179
  430.1 5.9 %all-to-all-start.7 = ((bf16[2,32,4,128]{3,2,0,1:T(4,128)(2,1)}), bf16[2,32,4,128]{3,2,0,1:T(4,128)(2,1)S(1)}, u32[]{:S(2)}, u32[]{:S(2)}) async-start(bf16[2,32,4,128]{3,2,0,1:T(4,128)(2,1)} %dynamic-slice_convert_fusion), calls=%async_computation.7 | async-start | bytes 131072 | tf_op jit(solution)/shard_map/all_to_all | solution.py:183
  436.0 4.7 %all-to-all-start.6 = ((bf16[2,32,4,128]{3,2,0,1:T(4,128)(2,1)}), bf16[2,32,4,128]{3,2,0,1:T(4,128)(2,1)S(1)}, u32[]{:S(2)}, u32[]{:S(2)}) async-start(bf16[2,32,4,128]{3,2,0,1:T(4,128)(2,1)} %dynamic-slice_convert_fusion.1), calls=%async_computation.6 | async-start | bytes 131072 | tf_op jit(solution)/shard_map/all_to_all | solution.py:182
where the time goes:
time: 443 us; the launch traced here: 441 us
  blocking collectives  347 us (78%)
  starting transfers between devices  28.6 us (6%)
  matrix products  21.5 us (5%)
  local copies, waits for them, and re-layouts  21.1 us (5%)
  other arithmetic  19.5 us (4%)
    unnamed x1, blocking collectives  182 us
    all_gather x4, blocking collectives, folded(): lax.all_gather(part, axis, axis=dim, tiled=True)  166 us
  transfers between devices with their start and end apart: 8, of which 1 were waited for; matrix products, arithmetic and copies ran while one was open for 13% of the time, Pallas kernels for 0%

commit v1 on v0

v1 whole, which is shorter than its diff:
```python
from functools import partial

import jax
import jax.numpy as jnp
from jax import lax
from jax.experimental import pallas as pl
from jax.experimental.pallas import tpu as pltpu
from jax.sharding import PartitionSpec as P

MESH = pl.DeviceIdType.MESH
masked_score = -1e30
F32, BF16 = jnp.float32, jnp.bfloat16


def dot(a, b, dims=((1,), (0,))):
    return lax.dot_general(a, b, (dims, ((), ())), preferred_element_type=F32)


def halves(x):
    high = x.astype(BF16)
    return high, (x - high.astype(F32)).astype(BF16)


def kernel(
    sizes,
    qg_ref,
    kv_ref,
    og_ref,
    okv_ref,
    qgb,
    kvb,
    out_qg,
    acc,
    recv,
    out_kv,
    wide,
    turned,
    kv_s,
    kv_r,
    qg_s,
    qg_r,
    z_s,
    z_r,
    p_s,
    p_r,
    o_s,
    o_r,
    f_s,
    f_r,
    local,
):
    layers, inner, outer, tp_n, t, heads, width = sizes
    G = inner * tp_n
    B = G * t
    T = outer * B
    rows = t * heads
    scale = width**-0.5
    ctx, tp = lax.axis_index("ctx"), lax.axis_index("tp")
    z = ctx // inner
    me = (ctx % inner) * tp_n + tp

    def in_plane(peer):
        return {"ctx": z * inner + peer // tp_n, "tp": peer % tp_n}

    def in_column(o):
        return {"ctx": o * inner + ctx % inner, "tp": tp}

    def kv_copy(l, to, slot):
        return pltpu.make_async_remote_copy(
            kv_ref.at[to, l], kvb.at[l, z, slot], kv_s.at[l, to], kv_r.at[l, slot], in_plane(to), MESH
        )

    def qg_copy(l, to, slot):
        return pltpu.make_async_remote_copy(
            qg_ref.at[to, l], qgb.at[l, slot], qg_s.at[l, to], qg_r.at[l, slot], in_plane(to), MESH
        )

    def z_copy(l, to, slot):
        return pltpu.make_async_remote_copy(
            kvb.at[l, slot], kvb.at[l, slot], z_s.at[l, to], z_r.at[l, slot], in_column(to), MESH
        )

    def p_copy(l, to, slot):
        return pltpu.make_async_remote_copy(
            acc.at[l, to], recv.at[l, slot], p_s.at[l, to], p_r.at[l, slot], in_column(to), MESH
        )

    def o_copy(l, to, slot):
        return pltpu.make_async_remote_copy(
            out_qg.at[l, to], og_ref.at[slot, l], o_s.at[l, to], o_r.at[l, slot], in_plane(to), MESH
        )

    def f_copy(l, to, slot):
        return pltpu.make_async_remote_copy(
            out_kv.at[l, to], okv_ref.at[slot, l], f_s.at[l, to], f_r.at[l, slot], in_plane(to), MESH
        )

    def each_peer(fn):
        for d in range(1, G):
            fn(lax.rem(me + d, G))

    barrier = pltpu.get_barrier_semaphore()
    each_peer(lambda p: pl.semaphore_signal(barrier, 1, device_id=in_plane(p), device_id_type=MESH))

    @pl.loop(1, outer)
    def _(d):
        pl.semaphore_signal(
            barrier, 1, device_id=in_column(lax.rem(z + d, outer)), device_id_type=MESH
        )

    pl.semaphore_wait(barrier, G - 1 + outer - 1)

    for l in range(layers):
        each_peer(lambda p: kv_copy(l, p, me).start())
    for l in range(layers):
        each_peer(lambda p: qg_copy(l, p, me).start())
    own = []
    for l in range(layers):
        own.append(pltpu.make_async_copy(kv_ref.at[me, l], kvb.at[l, z, me], local.at[l, 0]))
        own.append(pltpu.make_async_copy(qg_ref.at[me, l], qgb.at[l, me], local.at[l, 1]))
    for copy in own:
        copy.start()
    for l in range(layers):

        @pl.loop(z + 1, outer)
        def _(o):
            kvb[l, o] = jnp.zeros(kvb.shape[2:], BF16)

    for copy in own:
        copy.wait()
    for l in range(layers):
        each_peer(lambda p: kv_copy(l, me, p).wait_recv())

        @pl.loop(z + 1, outer)
        def _(o):
            z_copy(l, o, z).start()

    n = max(1, min(G, 256 // rows))
    c = n * rows

    def whole(l, kind):
        if t % 16 == 0:
            return kvb[l, :, :, kind].reshape(T, width)
        return wide[kind].reshape(T, width).astype(BF16)

    for l in range(layers):
        each_peer(lambda p: qg_copy(l, me, p).wait_recv())

        @pl.loop(0, z)
        def _(o):
            z_copy(l, me * 0 + o, o).wait_recv()

        if t % 16:

            @pl.loop(0, outer)
            def _(o):
                for p in range(G):
                    for kind in range(2):
                        wide[kind, o, p * t : (p + 1) * t, :] = kvb[l, o, p, kind].astype(F32)

        for kind in range(2):
            turned[kind] = whole(l, kind).astype(F32).T.astype(BF16)
        acc[l] = jnp.zeros(acc.shape[1:], F32)

        @pl.loop(0, G // n)
        def _(ci):
            K, V = whole(l, 0), whole(l, 1)
            span = pl.ds(ci * n, n)
            Q = qgb[l, span, 0].reshape(c, width)
            dO = qgb[l, span, 1].reshape(c, width)
            token = z * B + (ci * c + lax.broadcasted_iota(jnp.int32, (1, c), 1)) // heads
            allowed = lax.broadcasted_iota(jnp.int32, (T, c), 0) <= token
            scores = jnp.where(allowed, dot(K, Q, ((1,), (1,))) * scale, masked_score)
            e = jnp.exp(scores - jnp.max(scores, axis=0, keepdims=True))
            prob = e * (1.0 / jnp.sum(e, axis=0, keepdims=True))
            ph, pe = halves(prob)
            att = (dot(turned[1], ph) + dot(turned[1], pe)).T.astype(BF16)
            out_qg[l, span, 0] = att.reshape(n, rows, width)
            delta = jnp.sum((att.astype(F32) * dO.astype(F32)).T, axis=0, keepdims=True)
            dscore = prob * (dot(V, dO, ((1,), (1,))) - delta)
            dh, de = halves(dscore)
            dq = ((dot(turned[0], dh) + dot(turned[0], de)) * scale).T.astype(BF16)
            out_qg[l, span, 1] = dq.reshape(n, rows, width)
            acc[l, :, 0] += (dot(dh, Q) + dot(de, Q)).reshape(outer, B, width)
            acc[l, :, 1] += (dot(ph, dO) + dot(pe, dO)).reshape(outer, B, width)
            for i in range(n):
                peer = ci * n + i

                @pl.when(peer != me)
                def _():
                    o_copy(l, peer, me).start()

        @pl.loop(0, z)
        def _(o):
            p_copy(l, o, z).start()

        pltpu.make_async_copy(out_qg.at[l, me], og_ref.at[me, l], local.at[l, 2]).start()

    for l in range(layers):

        @pl.loop(z + 1, outer)
        def _(o):
            p_copy(l, z, o).wait_recv()
            acc[l, z] += recv[l, o]

        for kind in range(2):
            factor = scale if kind == 0 else 1.0
            for p in range(G):
                out_kv[l, p, kind] = (acc[l, z, kind, p * t : (p + 1) * t, :] * factor).astype(BF16)
        each_peer(lambda p: f_copy(l, p, me).start())
        pltpu.make_async_copy(out_kv.at[l, me], okv_ref.at[me, l], local.at[l, 3]).start()

    for l in range(layers):
        pltpu.make_async_copy(out_qg.at[l, me], og_ref.at[me, l], local.at[l, 2]).wait()
        pltpu.make_async_copy(out_kv.at[l, me], okv_ref.at[me, l], local.at[l, 3]).wait()

        def finish(p):
            kv_copy(l, p, me).wait_send()
            qg_copy(l, p, me).wait_send()
            o_copy(l, p, me).wait_send()
            f_copy(l, p, me).wait_send()
            o_copy(l, me, p).wait_recv()
            f_copy(l, me, p).wait_recv()

        each_peer(finish)

        @pl.loop(z + 1, outer)
        def _(o):
            z_copy(l, o, z).wait_send()

        @pl.loop(0, z)
        def _(o):
            p_copy(l, o, z).wait_send()


def on_device(q, k, v, g):
    layers, t, head_count, width = q.shape
    kv_heads = k.shape[2]
    heads = head_count // kv_heads
    ctx_n, tp_n = lax.axis_size("ctx"), lax.axis_size("tp")
    inner = kv_heads // tp_n
    outer = ctx_n // inner
    G, B, rows = kv_heads, kv_heads * t, t * heads

    def pack(a, b):
        both = jnp.stack([a, b]).reshape(2, layers, t, kv_heads, -1, width)
        return both.transpose(3, 1, 0, 2, 4, 5).reshape(kv_heads, layers, 2, -1, width)

    def unpack(both):
        both = both.reshape(kv_heads, layers, 2, t, -1, width).transpose(2, 1, 3, 0, 4, 5)
        both = both.reshape(2, layers, t, -1, width)
        return both[0], both[1]

    vmem = pl.BlockSpec(memory_space=pltpu.VMEM)
    sem = pltpu.SemaphoreType.DMA
    plane, column = sem((layers, G)), sem((layers, outer))
    qg_shape = (kv_heads, layers, 2, rows, width)
    kv_shape = (kv_heads, layers, 2, t, width)
    og, okv = pl.pallas_call(
        partial(kernel, (layers, inner, outer, tp_n, t, heads, width)),
        out_shape=(jax.ShapeDtypeStruct(qg_shape, BF16), jax.ShapeDtypeStruct(kv_shape, BF16)),
        in_specs=[vmem, vmem],
        out_specs=(vmem, vmem),
        scratch_shapes=[
            pltpu.VMEM((layers, G, 2, rows, width), BF16),
            pltpu.VMEM((layers, outer, G, 2, t, width), BF16),
            pltpu.VMEM((layers, G, 2, rows, width), BF16),
            pltpu.VMEM((layers, outer, 2, B, width), F32),
            pltpu.VMEM((layers, outer, 2, B, width), F32),
            pltpu.VMEM((layers, G, 2, t, width), BF16),
            pltpu.VMEM((2, outer, B, width) if t % 16 else (2, 1, 8, width), F32),
            pltpu.VMEM((2, width, outer * B), BF16),
            plane,
            plane,
            plane,
            plane,
            column,
            column,
            column,
            column,
            plane,
            plane,
            plane,
            plane,
            sem((layers, 4)),
        ],
        compiler_params=pltpu.CompilerParams(collective_id=0, has_side_effects=True),
    )(pack(q, g), pack(k, v))
    attended, grad_query = unpack(og)
    grad_key, grad_value = unpack(okv)
    return attended, grad_query, grad_key, grad_value


def solution(mesh):
    spec = P(None, ("ctx", "tp"), None, None)
    return jax.shard_map(
        on_device, mesh=mesh, in_specs=(spec,) * 4, out_specs=(spec,) * 4, check_vma=False
    )
```

time: 443 us -> 61 us (0.14)
  blocking collectives: 347 us -> 0 us
  Pallas kernels: 0 us -> 50.8 us
  starting transfers between devices: 28.6 us -> 0 us
  matrix products: 21.5 us -> 0 us
  other arithmetic: 19.5 us -> 2.96 us
  local copies, waits for them, and re-layouts: 21.1 us -> 6.3 us
    unnamed x1 -> x0, blocking collectives: 182 us -> none
    all_gather x4 -> x0, blocking collectives: 166 us -> none  [folded(): lax.all_gather(part, axis, axis=dim, tiled=True)]
    pallas_call x0 -> x1, Pallas kernels: none -> 50.8 us  [on_device(): pl.pallas_call(partial(kernel, (layers, inner, outer, tp_n, t, heads, wid...]
    all_to_all x8 -> x0, starting transfers between devices: 28.6 us -> none  [the longest x1 4.23 us: on_device(): lax.all_to_all(as_sent(grad_query), 'tp', split_axis=1, concat_axis=2, ti...]
    dot_general x14 -> x0, matrix products: 21.5 us -> none  [the longest x2 4.76 us: update(): jnp.einsum('tkgn,nkd->tkgd', weights, value_piece.astype(jnp.float32), pr...]
    another operation x5 -> x0, other arithmetic: 8.21 us -> none  [the longest x1 4.12 us: on_device(): jnp.stack(key_parts)]
    unnamed x15 -> x4, local copies, waits for them, and re-layouts: 7.97 us -> 1.32 us
    all_to_all x5 -> x0, local copies, waits for them, and re-layouts: 5.35 us -> none  [the longest x1 1.92 us: on_device(): lax.all_to_all(as_sent(attended), 'tp', split_axis=1, concat_axis=2, tile...]
  transfers between devices with their start and end apart: 8 -> 0, of which waited for: 1 -> 0; matrix products, arithmetic and copies ran while one was open for 13% -> 0% of each run, Pallas kernels for 0% -> 0%
where the time goes in v1:
time: 61 us; the launch traced here: 60.7 us
  Pallas kernels  50.8 us (83%)
  local copies, waits for them, and re-layouts  6.3 us (10%)
  other arithmetic  2.96 us (5%)
  between operations  0.66 us (1%)
    pallas_call x1, Pallas kernels, on_device(): pl.pallas_call(partial(kernel, (layers, inner, outer, tp_n, t, heads, wid...  50.8 us
    slice x3, local copies, waits for them, and re-layouts, unpack(): return (both[0], both[1])  3.15 us
    reshape x2, other arithmetic, pack(): both.transpose(3, 1, 0, 2, 4, 5).reshape(kv_heads, layers, 2, -1, width)  2.96 us
    unnamed x4, local copies, waits for them, and re-layouts  1.32 us

profile of v1, /device:TPU:0, one launch (start us, length us, event | category | flops | bytes accessed | tf_op | source)
XLA Modules:
  0.0 60.7 jit_solution(7060725305585171520)
XLA Ops:
  0.6 0.0 copy-start
  0.6 0.9 %copy_bitcast_fusion.3 = (bf16[1,2,16,8,128]{4,2,0,1,3:T(8,128)(2,1)S(1)}, bf16[1,2,16,8,128]{4,2,0,1,3:T(8,128)(2,1)S(1)}) fusion(bf16[2,16,8,128]{3,2,1,0:T(8,128)(2,1)} %param.6, bf16[2,16,8,128]{3,2,1,0:T(8,128)(2,1)} %param.5), kind=kLoop, calls=%fused_computation.7 | loop fusion | bytes 262144 | tf_op jit(solution)/shard_map/stack | solution.py:246
  1.6 0.7 %maximum_bitcast_fusion.kv_ref = bf16[8,2,2,16,128]{4,3,2,1,0:T(8,128)(2,1)} fusion(bf16[1,2,16,8,128]{4,2,0,1,3:T(8,128)(2,1)S(1)} %get-tuple-element.16, bf16[1,2,16,8,128]{4,2,0,1,3:T(8,128)(2,1)S(1)} %get-tuple-element.17), kind=kLoop, calls=%fused_computation.4 | loop fusion | flops 65536 | bytes 262144 | tf_op jit(solution)/shard_map/reshape | solution.py:247
  2.3 0.0 copy-done
  2.3 2.3 %copy_bitcast_fusion.qg_ref = bf16[8,2,2,128,128]{4,3,2,1,0:T(8,128)(2,1)} fusion(bf16[1,2,16,8,8,128]{5,4,3,2,1,0:T(8,128)(2,1)S(1)} %bitcast.35, bf16[1,2,16,8,8,128]{5,4,3,2,1,0:T(8,128)(2,1)} %bitcast.36), kind=kLoop, calls=%fused_computation.1 | loop fusion | flops 524288 | bytes 2097152 | tf_op jit(solution)/shard_map/reshape | solution.py:247
  4.6 50.8 %shard_map.75 = (bf16[8,2,2,128,128]{4,3,2,1,0:T(8,128)(2,1)}, bf16[8,2,2,16,128]{4,3,2,1,0:T(8,128)(2,1)}) custom-call(bf16[8,2,2,128,128]{4,3,2,1,0:T(8,128)(2,1)} %copy_bitcast_fusion.qg_ref, bf16[8,2,2,16,128]{4,3,2,1,0:T(8,128)(2,1)} %maximum_bitcast_fusion.kv_ref), custom_call_target="tpu_custom_call" | custom-call | tf_op jit(solution)/shard_map/pallas_call | solution.py:259
  55.4 0.9 %slice_bitcast_fusion = (bf16[2,16,8,128]{3,1,0,2:T(8,128)(2,1)S(1)}, bf16[2,16,8,128]{3,1,0,2:T(8,128)(2,1)S(1)}) fusion(bf16[2,2,16,8,1,128]{5,2,0,1,3,4:T(8,128)(2,1)} %bitcast.37), kind=kLoop, calls=%fused_computation.5 | loop fusion | bytes 262144 | tf_op jit(solution)/shard_map/squeeze | solution.py:252
  56.3 0.7 %copy.15 = bf16[2,16,8,128]{3,2,1,0:T(8,128)(2,1)} copy(bf16[2,16,8,128]{3,1,0,2:T(8,128)(2,1)S(1)} %get-tuple-element.14) | data formatting | bytes 131072
  56.9 1.3 %fusion = (bf16[1,2,16,8,8,128]{5,4,2,0,1,3:T(8,128)(2,1)S(1)}, bf16[1,2,16,8,8,128]{5,4,2,0,1,3:T(8,128)(2,1)S(1)}) fusion(bf16[2,2,16,8,8,128]{5,4,2,0,1,3:T(8,128)(2,1)} %bitcast.32), kind=kLoop, calls=%fused_computation.9 | loop fusion | bytes 2097152 | tf_op jit(solution)/shard_map/slice | solution.py:252
  58.2 0.9 %copy.22 = bf16[1,2,16,8,8,128]{5,4,3,2,1,0:T(8,128)(2,1)} copy(bf16[1,2,16,8,8,128]{5,4,2,0,1,3:T(8,128)(2,1)S(1)} %get-tuple-element.12) | data formatting | bytes 1048576 | tf_op jit(solution)/shard_map/slice | solution.py:252
  59.1 0.7 %copy.14 = bf16[2,16,8,128]{3,2,1,0:T(8,128)(2,1)} copy(bf16[2,16,8,128]{3,1,0,2:T(8,128)(2,1)S(1)} %get-tuple-element.15) | data formatting | bytes 131072
  59.8 0.9 %copy.23 = bf16[1,2,16,8,8,128]{5,4,3,2,1,0:T(8,128)(2,1)} copy(bf16[1,2,16,8,8,128]{5,4,2,0,1,3:T(8,128)(2,1)S(1)} %get-tuple-element.13) | data formatting | bytes 1048576 | tf_op jit(solution)/shard_map/slice | solution.py:252
Async XLA Ops:
  0.6 1.6 %copy-start = (bf16[2,16,64,128]{3,2,1,0:T(8,128)(2,1)S(1)}, bf16[2,16,64,128]{3,2,1,0:T(8,128)(2,1)}, u32[]{:S(2)}) copy-start(bf16[2,16,64,128]{3,2,1,0:T(8,128)(2,1)} %param.7) | copy-start | bytes 1572868

commit v2 on v1

--- a/solution.py
+++ b/solution.py
@@ -23,9 +23,11 @@
 
 def kernel(
     sizes,
-    qg_ref,
+    q_ref,
+    g_ref,
     kv_ref,
-    og_ref,
+    att_ref,
+    dq_ref,
     okv_ref,
     qgb,
     kvb,
@@ -70,9 +72,17 @@
             kv_ref.at[to, l], kvb.at[l, z, slot], kv_s.at[l, to], kv_r.at[l, slot], in_plane(to), MESH
         )
 
-    def qg_copy(l, to, slot):
-        return pltpu.make_async_remote_copy(
-            qg_ref.at[to, l], qgb.at[l, slot], qg_s.at[l, to], qg_r.at[l, slot], in_plane(to), MESH
+    def group(ref, l, peer):
+        return ref.at[l, :, pl.ds(pl.multiple_of(peer * heads, heads), heads), :]
+
+    def qg_copy(l, kind, to, slot):
+        return pltpu.make_async_remote_copy(
+            group((q_ref, g_ref)[kind], l, to),
+            qgb.at[l, slot, kind],
+            qg_s.at[l, kind, to],
+            qg_r.at[l, kind, slot],
+            in_plane(to),
+            MESH,
         )
 
     def z_copy(l, to, slot):
@@ -85,9 +95,19 @@
             acc.at[l, to], recv.at[l, slot], p_s.at[l, to], p_r.at[l, slot], in_column(to), MESH
         )
 
-    def o_copy(l, to, slot):
-        return pltpu.make_async_remote_copy(
-            out_qg.at[l, to], og_ref.at[slot, l], o_s.at[l, to], o_r.at[l, slot], in_plane(to), MESH
+    def o_copy(l, kind, to, slot):
+        return pltpu.make_async_remote_copy(
+            out_qg.at[l, to, kind],
+            group((att_ref, dq_ref)[kind], l, slot),
+            o_s.at[l, kind, to],
+            o_r.at[l, kind, slot],
+            in_plane(to),
+            MESH,
+        )
+
+    def o_own(l, kind):
+        return pltpu.make_async_copy(
+            out_qg.at[l, me, kind], group((att_ref, dq_ref)[kind], l, me), local.at[l, 3 + kind]
         )
 
     def f_copy(l, to, slot):
@@ -113,11 +133,15 @@
     for l in range(layers):
         each_peer(lambda p: kv_copy(l, p, me).start())
     for l in range(layers):
-        each_peer(lambda p: qg_copy(l, p, me).start())
+        for kind in range(2):
+            each_peer(lambda p: qg_copy(l, kind, p, me).start())
     own = []
     for l in range(layers):
         own.append(pltpu.make_async_copy(kv_ref.at[me, l], kvb.at[l, z, me], local.at[l, 0]))
-        own.append(pltpu.make_async_copy(qg_ref.at[me, l], qgb.at[l, me], local.at[l, 1]))
+        for kind, ref in enumerate((q_ref, g_ref)):
+            own.append(
+                pltpu.make_async_copy(group(ref, l, me), qgb.at[l, me, kind], local.at[l, 1 + kind])
+            )
     for copy in own:
         copy.start()
     for l in range(layers):
@@ -144,7 +168,8 @@
         return wide[kind].reshape(T, width).astype(BF16)
 
     for l in range(layers):
-        each_peer(lambda p: qg_copy(l, me, p).wait_recv())
+        for kind in range(2):
+            each_peer(lambda p: qg_copy(l, kind, me, p).wait_recv())
 
         @pl.loop(0, z)
         def _(o):
@@ -175,12 +200,12 @@
             prob = e * (1.0 / jnp.sum(e, axis=0, keepdims=True))
             ph, pe = halves(prob)
             att = (dot(turned[1], ph) + dot(turned[1], pe)).T.astype(BF16)
-            out_qg[l, span, 0] = att.reshape(n, rows, width)
+            out_qg[l, span, 0] = att.reshape(n, t, heads, width)
             delta = jnp.sum((att.astype(F32) * dO.astype(F32)).T, axis=0, keepdims=True)
             dscore = prob * (dot(V, dO, ((1,), (1,))) - delta)
             dh, de = halves(dscore)
             dq = ((dot(turned[0], dh) + dot(turned[0], de)) * scale).T.astype(BF16)
-            out_qg[l, span, 1] = dq.reshape(n, rows, width)
+            out_qg[l, span, 1] = dq.reshape(n, t, heads, width)
             acc[l, :, 0] += (dot(dh, Q) + dot(de, Q)).reshape(outer, B, width)
             acc[l, :, 1] += (dot(ph, dO) + dot(pe, dO)).reshape(outer, B, width)
             for i in range(n):
@@ -188,13 +213,15 @@
 
                 @pl.when(peer != me)
                 def _():
-                    o_copy(l, peer, me).start()
+                    for kind in range(2):
+                        o_copy(l, kind, peer, me).start()
 
         @pl.loop(0, z)
         def _(o):
             p_copy(l, o, z).start()
 
-        pltpu.make_async_copy(out_qg.at[l, me], og_ref.at[me, l], local.at[l, 2]).start()
+        for kind in range(2):
+            o_own(l, kind).start()
 
     for l in range(layers):
 
@@ -208,18 +235,20 @@
             for p in range(G):
                 out_kv[l, p, kind] = (acc[l, z, kind, p * t : (p + 1) * t, :] * factor).astype(BF16)
         each_peer(lambda p: f_copy(l, p, me).start())
-        pltpu.make_async_copy(out_kv.at[l, me], okv_ref.at[me, l], local.at[l, 3]).start()
-
-    for l in range(layers):
-        pltpu.make_async_copy(out_qg.at[l, me], og_ref.at[me, l], local.at[l, 2]).wait()
-        pltpu.make_async_copy(out_kv.at[l, me], okv_ref.at[me, l], local.at[l, 3]).wait()
+        pltpu.make_async_copy(out_kv.at[l, me], okv_ref.at[me, l], local.at[l, 5]).start()
+
+    for l in range(layers):
+        for kind in range(2):
+            o_own(l, kind).wait()
+        pltpu.make_async_copy(out_kv.at[l, me], okv_ref.at[me, l], local.at[l, 5]).wait()
 
         def finish(p):
             kv_copy(l, p, me).wait_send()
-            qg_copy(l, p, me).wait_send()
-            o_copy(l, p, me).wait_send()
+            for kind in range(2):
+                qg_copy(l, kind, p, me).wait_send()
+                o_copy(l, kind, p, me).wait_send()
+                o_copy(l, kind, me, p).wait_recv()
             f_copy(l, p, me).wait_send()
-            o_copy(l, me, p).wait_recv()
             f_copy(l, me, p).wait_recv()
 
         each_peer(finish)
@@ -240,7 +269,7 @@
     ctx_n, tp_n = lax.axis_size("ctx"), lax.axis_size("tp")
     inner = kv_heads // tp_n
     outer = ctx_n // inner
-    G, B, rows = kv_heads, kv_heads * t, t * heads
+    G, B = kv_heads, kv_heads * t
 
     def pack(a, b):
         both = jnp.stack([a, b]).reshape(2, layers, t, kv_heads, -1, width)
@@ -254,17 +283,18 @@
     vmem = pl.BlockSpec(memory_space=pltpu.VMEM)
     sem = pltpu.SemaphoreType.DMA
     plane, column = sem((layers, G)), sem((layers, outer))
-    qg_shape = (kv_heads, layers, 2, rows, width)
+    pair = sem((layers, 2, G))
+    whole_shape = jax.ShapeDtypeStruct(q.shape, BF16)
     kv_shape = (kv_heads, layers, 2, t, width)
-    og, okv = pl.pallas_call(
+    attended, grad_query, okv = pl.pallas_call(
         partial(kernel, (layers, inner, outer, tp_n, t, heads, width)),
-        out_shape=(jax.ShapeDtypeStruct(qg_shape, BF16), jax.ShapeDtypeStruct(kv_shape, BF16)),
-        in_specs=[vmem, vmem],
-        out_specs=(vmem, vmem),
+        out_shape=(whole_shape, whole_shape, jax.ShapeDtypeStruct(kv_shape, BF16)),
+        in_specs=[vmem, vmem, vmem],
+        out_specs=(vmem, vmem, vmem),
         scratch_shapes=[
-            pltpu.VMEM((layers, G, 2, rows, width), BF16),
+            pltpu.VMEM((layers, G, 2, t, heads, width), BF16),
             pltpu.VMEM((layers, outer, G, 2, t, width), BF16),
-            pltpu.VMEM((layers, G, 2, rows, width), BF16),
+            pltpu.VMEM((layers, G, 2, t, heads, width), BF16),
             pltpu.VMEM((layers, outer, 2, B, width), F32),
             pltpu.VMEM((layers, outer, 2, B, width), F32),
             pltpu.VMEM((layers, G, 2, t, width), BF16),
@@ -272,21 +302,20 @@
             pltpu.VMEM((2, width, outer * B), BF16),
             plane,
             plane,
-            plane,
-            plane,
+            pair,
+            pair,
             column,
             column,
             column,
             column,
+            pair,
+            pair,
             plane,
             plane,
-            plane,
-            plane,
-            sem((layers, 4)),
+            sem((layers, 6)),
         ],
         compiler_params=pltpu.CompilerParams(collective_id=0, has_side_effects=True),
-    )(pack(q, g), pack(k, v))
-    attended, grad_query = unpack(og)
+    )(q, g, pack(k, v))
     grad_key, grad_value = unpack(okv)
     return attended, grad_query, grad_key, grad_value
 

time: 61 us -> 58.4 us (0.957)
  other arithmetic: 2.96 us -> 0.67 us
  local copies, waits for them, and re-layouts: 6.3 us -> 5.17 us
    slice x3 -> x0, local copies, waits for them, and re-layouts: 3.15 us -> none  [unpack(): return (both[0], both[1])]
    reshape x2 -> x1, other arithmetic: 2.96 us -> 0.67 us  [pack(): both.transpose(3, 1, 0, 2, 4, 5).reshape(kv_heads, layers, 2, -1, width)]
    unnamed x4 -> x8, local copies, waits for them, and re-layouts: 1.32 us -> 3.34 us
where the time goes in v2:
time: 58.4 us; the launch traced here: 57.8 us
  Pallas kernels  51.3 us (88%)
  local copies, waits for them, and re-layouts  5.17 us (9%)
  other arithmetic  0.67 us (1%)
  between operations  0.66 us (1%)
    pallas_call x1, Pallas kernels, on_device(): pl.pallas_call(partial(kernel, (layers, inner, outer, tp_n, t, heads, wid...  51.3 us
    unnamed x8, local copies, waits for them, and re-layouts  3.34 us

profile of v2, /device:TPU:0, one launch (start us, length us, event | category | flops | bytes accessed | tf_op | source)
XLA Modules:
  0.0 57.8 jit_solution(3849323924923478158)
XLA Ops:
  0.6 0.9 %copy_bitcast_fusion = (bf16[1,2,16,8,128]{4,2,0,1,3:T(8,128)(2,1)S(1)}, bf16[1,2,16,8,128]{4,2,0,1,3:T(8,128)(2,1)S(1)}) fusion(bf16[2,16,8,128]{3,2,1,0:T(8,128)(2,1)} %param.6, bf16[2,16,8,128]{3,2,1,0:T(8,128)(2,1)} %param.5), kind=kLoop, calls=%fused_computation.3 | loop fusion | bytes 262144 | tf_op jit(solution)/shard_map/stack | solution.py:275
  1.5 0.7 %maximum_bitcast_fusion.kv_ref = bf16[8,2,2,16,128]{4,3,2,1,0:T(8,128)(2,1)} fusion(bf16[1,2,16,8,128]{4,2,0,1,3:T(8,128)(2,1)S(1)} %get-tuple-element.16, bf16[1,2,16,8,128]{4,2,0,1,3:T(8,128)(2,1)S(1)} %get-tuple-element.17), kind=kLoop, calls=%fused_computation | loop fusion | flops 65536 | bytes 262144 | tf_op jit(solution)/shard_map/reshape | solution.py:276
  2.2 51.3 %shard_map.75 = (bf16[2,16,64,128]{3,2,1,0:T(8,128)(2,1)}, bf16[2,16,64,128]{3,2,1,0:T(8,128)(2,1)}, bf16[8,2,2,16,128]{4,3,2,1,0:T(8,128)(2,1)}) custom-call(bf16[2,16,64,128]{3,2,1,0:T(8,128)(2,1)} %q_ref.1, bf16[2,16,64,128]{3,2,1,0:T(8,128)(2,1)} %g_ref.1, bf16[8,2,2,16,128]{4,3,2,1,0:T(8,128)(2,1)} %maximum_bitcast_fusion.kv_ref), custom_call_target="tpu_custom_call" | custom-call | tf_op jit(solution)/shard_map/pallas_call | solution.py:289
  53.5 0.0 copy-start.1
  53.5 0.9 %slice_bitcast_fusion = (bf16[2,16,8,128]{3,1,0,2:T(8,128)(2,1)S(1)}, bf16[2,16,8,128]{3,1,0,2:T(8,128)(2,1)S(1)}) fusion(bf16[2,2,16,8,1,128]{5,2,0,1,3,4:T(8,128)(2,1)} %bitcast.17), kind=kLoop, calls=%fused_computation.1 | loop fusion | bytes 262144 | tf_op jit(solution)/shard_map/squeeze | solution.py:281
  54.4 0.7 %copy.11 = bf16[2,16,8,128]{3,2,1,0:T(8,128)(2,1)} copy(bf16[2,16,8,128]{3,1,0,2:T(8,128)(2,1)S(1)} %get-tuple-element.14) | data formatting | bytes 131072
  55.1 0.7 %copy.10 = bf16[2,16,8,128]{3,2,1,0:T(8,128)(2,1)} copy(bf16[2,16,8,128]{3,1,0,2:T(8,128)(2,1)S(1)} %get-tuple-element.15) | data formatting | bytes 131072
  55.8 0.0 copy-done.1
  55.8 0.0 copy-start
  55.8 0.8 %copy.16 = bf16[2,16,64,128]{3,2,1,0:T(8,128)(2,1)} copy(bf16[2,16,64,128]{3,2,1,0:T(8,128)(2,1)S(1)} %copy-done.1) | data formatting | bytes 1048576
  56.6 0.4 copy-done
  57.0 0.8 %copy.17 = bf16[2,16,64,128]{3,2,1,0:T(8,128)(2,1)} copy(bf16[2,16,64,128]{3,2,1,0:T(8,128)(2,1)S(1)} %copy-done) | data formatting | bytes 1048576
Async XLA Ops:
  53.5 2.3 %copy-start.1 = (bf16[2,16,64,128]{3,2,1,0:T(8,128)(2,1)S(1)}, bf16[2,16,64,128]{3,2,1,0:T(8,128)(2,1)}, u32[]{:S(2)}) copy-start(bf16[2,16,64,128]{3,2,1,0:T(8,128)(2,1)} %get-tuple-element.22) | copy-start | bytes 1572868
  55.8 1.2 %copy-start = (bf16[2,16,64,128]{3,2,1,0:T(8,128)(2,1)S(1)}, bf16[2,16,64,128]{3,2,1,0:T(8,128)(2,1)}, u32[]{:S(2)}) copy-start(bf16[2,16,64,128]{3,2,1,0:T(8,128)(2,1)} %get-tuple-element.23) | copy-start | bytes 1572868
